TPU v7x, 32 devices: a whole 2x2x4 slice. The times are simulated.
32 devices in a mesh: groups: 2 (over x), row: 8 (over z, y), head: 2 (over core).
Axes of the slice: x: 2, y: 2, z: 4, core: 2. Of those that a mesh axis runs over, the one named last changes fastest.
Arguments:
- hidden: bfloat16 [48, 4096], P('groups'), parts along dimension 0, may hold values from -6 to 6
- norm_gain: float32 [4096], replicated, may hold values from 0.1 to 1.9
- w_query: bfloat16 [8, 256, 4096], P('head', 'row'), may hold values from -0.09375 to 0.09375
- w_key: bfloat16 [8, 256, 4096], P('head', 'row'), may hold values from -0.09375 to 0.09375
- w_value: bfloat16 [8, 512, 4096], P('head', 'row'), may hold values from -0.09375 to 0.09375
- w_outgate: bfloat16 [8, 512, 4096], P('head', 'row'), may hold values from -0.09375 to 0.09375
- w_out: bfloat16 [8, 512, 4096], P('head', 'row'), may hold values from -0.125 to 0.125
- w_gates: bfloat16 [2, 8, 4096], P(None, 'head'), may hold values from -0.09375 to 0.09375
- gate_bias: float32 [2, 8], P(None, 'head'), may hold values from -2 to 4
- headnorm_gain: float32 [8, 512], P('head', 'row'), may hold values from 0.1 to 1.9
- final_gain: float32 [4096], replicated, may hold values from 0.1 to 1.9
- w_vocab: bfloat16 [25152, 4096], P(('row', 'head')), may hold values from -39.0625 to 39.0625
- memory: float32 [48, 8, 256, 512], P('groups', 'head', 'row'), parts along dimension 0, may hold values from -6 to 6
- normalizer: float32 [48, 8, 256], P('groups', 'head', 'row'), parts along dimension 0, may hold values from -6 to 6
- stabilizer: float32 [48, 8], P('groups', 'head'), parts along dimension 0, may hold values from -2 to 2
- targets: int32 [48], P('groups'), parts along dimension 0, may hold values from 0 to 25151
Outputs:
- memory_out: float32 [48, 8, 256, 512], P('groups', 'head', 'row'), parts along dimension 0
- normalizer_out: float32 [48, 8, 256], P('groups', 'head', 'row'), parts along dimension 0
- stabilizer_out: float32 [48, 8], P('groups', 'head'), parts along dimension 0
- hidden_out: bfloat16 [48, 4096], P('groups', ('row', 'head')), parts along dimension 0
- log_prob: float32 [48], P('groups'), parts along dimension 0
There are 2 independent parts, one for each index of `groups`. A program takes and returns all parts, laid end to end along the dimension named above; an argument that names none is the same for every part. Nothing has to cross between parts.
All inputs are finite; a program needn't handle non-finite values.
Results may differ from a plain program's by a relative error of at most 0.0035.
The roundings to bfloat16 on the way count: a program that leaves them out, or rounds other values in their place, can miss the bound.
Values may be sent and summed in bfloat16 or wider, within the bound.
A program may use at most 64 MiB of HBM per device.

v0:
```python
import math
import jax
import jax.numpy as jnp
from jax import lax
from jax.sharding import PartitionSpec as P

QK_DIM = 256
epsilon = 1e-06


def joined_2(value, axis, join):
    pieces = jax.tree.map(lambda part: lax.all_gather(part, axis), value)
    head = jax.tree.map(lambda part: part[0], pieces)
    tail = jax.tree.map(lambda part: part[1:], pieces)
    total, _ = lax.scan(lambda total, share: (join(total, share), None), head, tail)
    return total


def rms_round(stream, gain):
    scale = lax.rsqrt(jnp.mean(stream * stream, axis=-1, keepdims=True) + epsilon)
    return (stream * scale * gain).astype(jnp.bfloat16)


def per_device(
    hidden,
    norm_gain,
    w_query,
    w_key,
    w_value,
    w_outgate,
    w_out,
    w_gates,
    gate_bias,
    headnorm_gain,
    final_gain,
    w_vocab,
    memory,
    normalizer,
    stabilizer,
    targets,
):
    value_rows = w_value.shape[1]
    stream = hidden.astype(jnp.float32)
    normed_in = rms_round(stream, norm_gain)

    def project(weights):
        return jnp.einsum("sd,hjd->shj", normed_in, weights, preferred_element_type=jnp.float32)

    queries = project(w_query) / math.sqrt(QK_DIM)
    key_part = project(w_key)
    value_part = project(w_value).astype(jnp.bfloat16)
    outgate_pre = project(w_outgate)
    gate_pre = (
        jnp.einsum("sd,ghd->gsh", normed_in, w_gates, preferred_element_type=jnp.float32)
        + gate_bias[:, None, :]
    )
    log_forget = jax.nn.log_sigmoid(gate_pre[1])
    stabilizer_out = jnp.maximum(log_forget + stabilizer, gate_pre[0])
    decay_rate = jnp.exp(log_forget + stabilizer - stabilizer_out)
    inflow = jnp.exp(gate_pre[0] - stabilizer_out)
    scaled_key = inflow[:, :, None] * key_part
    memory_out = (
        decay_rate[:, :, None, None] * memory
        + scaled_key[:, :, :, None]
        * lax.all_gather(value_part, "row", axis=2, tiled=True).astype(jnp.float32)[:, :, None, :]
    )
    normalizer_out = decay_rate[:, :, None] * normalizer + scaled_key
    partial_readout = jnp.einsum(
        "shj,shje->she", queries, memory_out, precision=lax.Precision.HIGHEST
    )
    readout = lax.psum(partial_readout, "row")
    average = jnp.mean(readout, axis=-1)
    centered_full = readout - average[:, :, None]
    variance = jnp.mean(centered_full * centered_full, axis=-1)
    centered = lax.dynamic_slice_in_dim(
        centered_full, lax.axis_index("row") * value_rows, value_rows, 2
    )
    normed = centered * lax.rsqrt(variance + epsilon)[:, :, None] * headnorm_gain
    gated_out = (jax.nn.sigmoid(outgate_pre) * normed).astype(jnp.bfloat16)
    partial_terms = jnp.einsum("shj,hjd->sd", gated_out, w_out, preferred_element_type=jnp.float32)
    position = lax.axis_index("row") * lax.axis_size("head") + lax.axis_index("head")
    share_width = hidden.shape[1] // (lax.axis_size("row") * lax.axis_size("head"))
    vocab_here = w_vocab.shape[0]
    projection = lax.psum(partial_terms, ("row", "head"))
    new_full = (stream + projection).astype(jnp.bfloat16)
    final_feat = rms_round(new_full.astype(jnp.float32), final_gain)
    logits = jnp.einsum("sd,vd->sv", final_feat, w_vocab, preferred_element_type=jnp.float32)
    hidden_out = lax.dynamic_slice_in_dim(new_full, position * share_width, share_width, 1)
    local_ids = targets - position * vocab_here
    is_target = jnp.arange(vocab_here, dtype=jnp.int32)[None, :] == local_ids[:, None]
    target_term = jnp.sum(jnp.where(is_target, logits, 0.0), axis=-1)
    local_max = jnp.max(logits, axis=-1)
    local_sum = jnp.sum(jnp.exp(logits - local_max[:, None]), axis=-1)

    def combine(earlier, later):
        highest = jnp.maximum(earlier[0], later[0])
        joined = earlier[1] * jnp.exp(earlier[0] - highest) + later[1] * jnp.exp(later[0] - highest)
        return (highest, joined, earlier[2] + later[2])

    highest, exp_total, picked = joined_2(
        (local_max, local_sum, target_term), ("row", "head"), combine
    )
    log_prob = picked - (highest + jnp.log(exp_total))
    return (memory_out, normalizer_out, stabilizer_out, hidden_out, log_prob)


def solution(mesh):
    in_specs = (
        P("groups", None),
        P(),
        P("head", "row", None),
        P("head", "row", None),
        P("head", "row", None),
        P("head", "row", None),
        P("head", "row", None),
        P(None, "head", None),
        P(None, "head"),
        P("head", "row"),
        P(),
        P(("row", "head"), None),
        P("groups", "head", "row", None),
        P("groups", "head", "row"),
        P("groups", "head"),
        P("groups"),
    )
    out_specs = (
        P("groups", "head", "row", None),
        P("groups", "head", "row"),
        P("groups", "head"),
        P("groups", ("row", "head")),
        P("groups"),
    )
    return jax.shard_map(
        per_device, mesh=mesh, in_specs=in_specs, out_specs=out_specs, check_vma=False
    )
```

profile of v0, /device:TPU:0, one launch (start us, length us, event | category | flops | bytes accessed | tf_op | source)
XLA Modules:
  0.0 280.0 jit_solution(1592682969917463788)
XLA Ops:
  7.2 0.0 copy-start
  7.2 0.0 all-reduce.7.cloned.1.call-start
  7.2 1.2 fusion.17
  8.5 2.7 convolution_convert_fusion
  11.1 0.1 copy.34
  11.3 33.0 %all_gather.21 = bf16[24,4,512]{0,1,2:T(4,128)(2,1)S(1)} all-gather(bf16[24,4,64]{0,1,2:T(4,128)(2,1)S(1)} %copy.34), channel_id=1, replica_groups=mesh['groups'=2,'row'=8,'head'=2] {'row'}, dimensions={2}, use_global_device_ids=true | all-gather | bytes 110592 | tf_op jit(solution)/shard_map/all_gather | solution.py:65
  44.3 0.3 copy.35
  44.6 0.1 copy.36
  44.7 1.2 fusion.13
  45.9 0.7 subtract_exponential_fusion.1
  46.6 0.0 copy-start.5
  46.6 0.1 copy.32
  46.7 2.2 fusion.28
  48.9 2.2 fusion.7
  51.1 3.4 %multiply_add_fusion = f32[24,4,32,512]{3,2,1,0:T(8,128)S(1)} fusion(f32[24,4,32,512]{3,2,1,0:T(8,128)} %param.30, f32[24,4,512]{2,1,0:T(4,128)S(1)} %copy.36, f32[24,4,32]{2,1,0:T(4,128)S(1)} %copy.33, f32[24,4]{1,0:T(8,128)S(1)} %copy.32), kind=kLoop, calls=%fused_computation.10 | loop fusion | flops 4718592 | bytes 12792192 | tf_op jit(solution)/shard_map/add | solution.py:63
  54.5 0.0 copy-done.5
  54.5 0.0 copy-start.1
  54.5 2.7 copy-done.1
  57.2 0.0 copy-start.8
  57.2 0.0 copy-start.2
  57.2 0.0 copy-start.3
  57.2 0.0 copy-start.6
  57.2 0.0 copy-start.7
  57.2 0.0 copy-start.4
  57.2 3.1 %fusion.26 = f32[24,4,1,512]{3,2,1,0:T(1,128)S(1)} fusion(f32[24,4,32,512]{3,2,1,0:T(8,128)S(1)} %multiply_add_fusion, f32[24,4,32,1]{2,0,1,3:T(8,128)S(1)} %fusion.7), kind=kOutput, calls=%fused_computation.46 | convolution fusion | flops 18874368 | bytes 6500352 | tf_op jit(solution)/shard_map/shj,shje->she/dot_general | solution.py:68
  60.4 0.7 copy.47
  61.1 0.0 all-reduce.7.cloned.1.call-update
  61.1 0.0 all-reduce.9.cloned.1.call-start
  61.2 0.6 copy.38
  61.8 0.0 copy-done.8
  61.8 0.6 dynamic-slice
  63.1 70.0 %all-reduce.7.cloned.1.call-done = f32[24,4,512]{2,0,1:T(8,128)} async-done(((f32[24,4,512]{2,0,1:T(8,128)}), f32[24,4,512]{2,0,1:T(8,128)}) %all-reduce.7.cloned.1.call-update) | async-done | bytes 196624 | tf_op jit(solution)/shard_map/psum | solution.py:71
  133.1 1.0 reduce_sum.55
  134.1 1.1 multiply_reduce_fusion
  135.2 0.0 copy-done
  135.2 0.0 copy-done.2
  135.2 0.0 copy-done.3
  135.2 0.0 copy-done.6
  135.3 3.8 %convolution_bitcast_fusion = f32[24,4096]{1,0:T(8,128)} fusion(bf16[4,64,4096]{2,1,0:T(8,128)(2,1)S(1)} %copy-done, bf16[4,64,4096]{2,1,0:T(8,128)(2,1)} %param.23, f32[24,4,512]{2,0,1:T(8,128)S(1)} %get-tuple-element.86, s32[]{:T(128)S(6)} %select_n.16, f32[4,64]{1,0:T(4,128)S(1)} %copy-done.6, f32[24,4]{0,1:T(4,128)S(1)} %add_rsqrt_fusion, ...), kind=kOutput, calls=%fused_computation.11 | convolution fusion | flops 101099520 | bytes 4854276 | tf_op jit(solution)/shard_map/shj,hjd->sd/dot_general | solution.py:80
  139.0 0.0 all-reduce.9.cloned.1.call-update
  139.0 0.0 copy-done.7
  139.1 90.6 %all-reduce.9.cloned.1.call-done = f32[24,4096]{1,0:T(8,128)} async-done(((f32[24,4096]{1,0:T(8,128)}), f32[24,4096]{1,0:T(8,128)}) %all-reduce.9.cloned.1.call-update) | async-done | bytes 393232 | tf_op jit(solution)/shard_map/psum | solution.py:84
  229.6 1.2 fusion.14
  230.8 0.0 copy-done.4
  230.8 8.3 %fusion.50 = (f32[24]{0:T(128)S(1)}, f32[24,1572]{1,0:T(8,128)S(1)}) fusion(bf16[1572,4096]{1,0:T(8,128)(2,1)} %param.29, bf16[24,4096]{1,0:T(8,128)(2,1)S(1)} %get-tuple-element.84, f32[4096]{0:T(1024)S(1)} %copy-done.4, f32[24]{0:T(128)S(1)} %add_rsqrt_fusion.1), kind=kOutput, calls=%fused_computation.74 | convolution fusion | flops 309498688 | bytes 13241920 | tf_op jit(solution)/shard_map/sd,vd->sv/dot_general | solution.py:87
  239.1 0.2 dynamic-update-slice
  239.3 0.2 select_reduce_fusion
  239.6 0.2 dynamic-update-slice.1
  239.8 0.2 dynamic-update-slice.2
  240.0 30.9 %all-reduce.3 = (f32[384]{0:T(512)S(1)}, f32[384]{0:T(512)S(1)}, f32[384]{0:T(512)S(1)}) all-reduce(f32[384]{0:T(512)S(1)} %dynamic-update-slice, f32[384]{0:T(512)S(1)} %dynamic-update-slice.1, f32[384]{0:T(512)S(1)} %dynamic-update-slice.2), channel_id=2, replica_groups=mesh['groups'=2,'row'=8,'head'=2] {'row','head'}, use_global_device_ids=true, to_apply=%add | all-reduce | flops 1152 | bytes 9216
  271.0 0.1 slice.36
  271.0 0.1 slice.37
  271.1 0.1 slice.38
  271.2 0.6 constant_dynamic-slice_fusion.3
  271.8 0.1 reshape.55
  271.9 0.1 reshape.56
  271.9 0.1 reshape.57
  272.0 0.6 while.14
  272.7 0.5 add_subtract_fusion
  (28 shorter events, 0.5 us)
Async XLA Ops:
  7.2 128.1 %copy-start = (bf16[4,64,4096]{2,1,0:T(8,128)(2,1)S(1)}, bf16[4,64,4096]{2,1,0:T(8,128)(2,1)}, u32[]{:S(2)}) copy-start(bf16[4,64,4096]{2,1,0:T(8,128)(2,1)} %param.24) | copy-start | bytes 6291460
  7.2 125.9 %all-reduce.7.cloned.1.call-start = ((), (), s32[]{:S(2)}) async-start(), calls=%async_computation | async-start | bytes 393216 | tf_op jit(solution)/shard_map/psum | solution.py:71
  46.6 7.9 %copy-start.5 = (f32[24,4]{0,1:T(4,128)}, f32[24,4]{0,1:T(4,128)S(1)}, u32[]{:S(2)}) copy-start(f32[24,4]{0,1:T(4,128)S(1)} %get-tuple-element.88) | copy-start | bytes 1156
  54.5 2.7 copy-start.1
  57.2 4.6 %copy-start.8 = (u32[32]{0:T(128)S(1)}, u32[32]{0:T(128)}, u32[]{:S(2)}) copy-start(u32[32]{0:T(128)} %constant.57) | copy-start | bytes 388
  57.2 78.0 %copy-start.2 = (bf16[24,4096]{1,0:T(8,128)(2,1)S(1)}, bf16[24,4096]{1,0:T(8,128)(2,1)}, u32[]{:S(2)}) copy-start(bf16[24,4096]{1,0:T(8,128)(2,1)} %param.18) | copy-start | bytes 589828
  57.2 78.0 %copy-start.3 = (f32[4096]{0:T(1024)S(1)}, f32[4096]{0:T(1024)}, u32[]{:S(2)}) copy-start(f32[4096]{0:T(1024)} %param.19) | copy-start | bytes 49156
  57.2 78.1 %copy-start.6 = (f32[4,64]{1,0:T(4,128)S(1)}, f32[4,64]{1,0:T(4,128)}, u32[]{:S(2)}) copy-start(f32[4,64]{1,0:T(4,128)} %param.27) | copy-start | bytes 3076
  57.2 81.8 %copy-start.7 = (s32[24]{0:T(128)S(1)}, s32[24]{0:T(128)}, u32[]{:S(2)}) copy-start(s32[24]{0:T(128)} %param.33) | copy-start | bytes 292
  57.2 173.6 %copy-start.4 = (f32[4096]{0:T(1024)S(1)}, f32[4096]{0:T(1024)}, u32[]{:S(2)}) copy-start(f32[4096]{0:T(1024)} %param.28) | copy-start | bytes 49156
  61.1 168.5 %all-reduce.9.cloned.1.call-start = ((), (), s32[]{:S(2)}) async-start(), calls=%async_computation.1 | async-start | bytes 786432 | tf_op jit(solution)/shard_map/psum | solution.py:84
Sparse Core Ops, SparseCore 0:
  61.2 71.7 all-reduce.6
  139.2 90.4 all-reduce.8
where the time goes:
time: 281 us; the launch traced here: 280 us
  waiting for transfers between devices  161 us (57%)
  blocking collectives  64 us (23%)
  matrix products  23.4 us (8%)
  between operations  15 us (5%)
  other arithmetic  9.78 us (3%)
  local copies, waits for them, and re-layouts  7.02 us (2%)
    psum x1, waiting for transfers between devices, per_device(): projection = lax.psum(partial_terms, ('row', 'head'))  90.6 us
    psum x1, waiting for transfers between devices, per_device(): readout = lax.psum(partial_readout, 'row')  70 us
    all_gather x1, blocking collectives, per_device(): lax.all_gather(value_part, 'row', axis=2, tiled=True).astype(jnp.float32)  33 us
    unnamed x1, blocking collectives  30.9 us
    dot_general x1, matrix products, per_device(): jnp.einsum('sd,vd->sv', final_feat, w_vocab, preferred_element_type=jnp.f...  8.26 us
    dot_general x3, matrix products, project(): jnp.einsum('sd,hjd->shj', normed_in, weights, preferred_element_type=jnp....  7.03 us
  transfers between devices with their start and end apart: 2, of which 2 were waited for; matrix products, arithmetic and copies ran while one was open for 0% of the time, Pallas kernels for 0%

commit v1 on v0

--- a/solution.py
+++ b/solution.py
@@ -81,7 +81,8 @@
     position = lax.axis_index("row") * lax.axis_size("head") + lax.axis_index("head")
     share_width = hidden.shape[1] // (lax.axis_size("row") * lax.axis_size("head"))
     vocab_here = w_vocab.shape[0]
-    projection = lax.psum(partial_terms, ("row", "head"))
+    connect_views = lambda mine_x: lax.psum(lax.psum(mine_x, axis_name="head"), "row")
+    projection = connect_views(partial_terms)
     new_full = (stream + projection).astype(jnp.bfloat16)
     final_feat = rms_round(new_full.astype(jnp.float32), final_gain)
     logits = jnp.einsum("sd,vd->sv", final_feat, w_vocab, preferred_element_type=jnp.float32)

time: 281 us -> 283 us (level)
  waiting for transfers between devices: 161 us -> 164 us
    psum x1 -> x2, waiting for transfers between devices: 90.6 us -> 92 us  [the longest x1 74.4 us: per_device(): lax.psum(lax.psum(mine_x, axis_name='head'), 'row')]
  transfers between devices with their start and end apart: 2 -> 3, of which waited for: 2 -> 3; matrix products, arithmetic and copies ran while one was open for 0% -> 0% of each run, Pallas kernels for 0% -> 0%
where the time goes in v1:
time: 283 us; the launch traced here: 282 us
  waiting for transfers between devices  164 us (58%)
  blocking collectives  63 us (22%)
  matrix products  23.4 us (8%)
  between operations  14.7 us (5%)
  other arithmetic  9.78 us (3%)
  local copies, waits for them, and re-layouts  7.02 us (2%)
    psum x1, waiting for transfers between devices, per_device(): lax.psum(lax.psum(mine_x, axis_name='head'), 'row')  74.4 us
    psum x1, waiting for transfers between devices, per_device(): readout = lax.psum(partial_readout, 'row')  71.9 us
    all_gather x1, blocking collectives, per_device(): lax.all_gather(value_part, 'row', axis=2, tiled=True).astype(jnp.float32)  33 us
    unnamed x1, blocking collectives  30 us
    psum x1, waiting for transfers between devices, per_device(): lax.psum(mine_x, axis_name='head')  17.6 us
    dot_general x1, matrix products, per_device(): jnp.einsum('sd,vd->sv', final_feat, w_vocab, preferred_element_type=jnp.f...  8.26 us
    dot_general x3, matrix products, project(): jnp.einsum('sd,hjd->shj', normed_in, weights, preferred_element_type=jnp....  7.03 us
  transfers between devices with their start and end apart: 3, of which 3 were waited for; matrix products, arithmetic and copies ran while one was open for 0% of the time, Pallas kernels for 0%

profile of v1, /device:TPU:0, one launch (start us, length us, event | category | flops | bytes accessed | tf_op | source)
XLA Modules:
  0.0 282.1 jit_solution(4863562200008397974)
XLA Ops:
  7.2 0.0 copy-start
  7.2 0.0 all-reduce.8.cloned.1.call-start
  7.2 1.2 fusion.17
  8.5 2.7 convolution_convert_fusion
  11.1 0.1 copy.34
  11.3 33.0 %all_gather.21 = bf16[24,4,512]{0,1,2:T(4,128)(2,1)S(1)} all-gather(bf16[24,4,64]{0,1,2:T(4,128)(2,1)S(1)} %copy.34), channel_id=1, replica_groups=mesh['groups'=2,'row'=8,'head'=2] {'row'}, dimensions={2}, use_global_device_ids=true | all-gather | bytes 110592 | tf_op jit(solution)/shard_map/all_gather | solution.py:65
  44.3 0.3 copy.35
  44.6 0.1 copy.36
  44.7 1.2 fusion.13
  45.9 0.7 subtract_exponential_fusion.1
  46.6 0.0 copy-start.5
  46.6 0.1 copy.32
  46.7 2.2 fusion.28
  48.9 2.2 fusion.7
  51.1 3.4 %multiply_add_fusion = f32[24,4,32,512]{3,2,1,0:T(8,128)S(1)} fusion(f32[24,4,32,512]{3,2,1,0:T(8,128)} %param.30, f32[24,4,512]{2,1,0:T(4,128)S(1)} %copy.36, f32[24,4,32]{2,1,0:T(4,128)S(1)} %copy.33, f32[24,4]{1,0:T(8,128)S(1)} %copy.32), kind=kLoop, calls=%fused_computation.10 | loop fusion | flops 4718592 | bytes 12792192 | tf_op jit(solution)/shard_map/add | solution.py:63
  54.5 0.0 copy-done.5
  54.5 0.0 copy-start.1
  54.5 2.7 copy-done.1
  57.2 0.0 copy-start.2
  57.2 0.0 copy-start.3
  57.2 0.0 copy-start.6
  57.2 0.0 copy-start.8
  57.2 0.0 copy-start.7
  57.2 0.0 copy-start.4
  57.2 3.1 %fusion.26 = f32[24,4,1,512]{3,2,1,0:T(1,128)S(1)} fusion(f32[24,4,32,512]{3,2,1,0:T(8,128)S(1)} %multiply_add_fusion, f32[24,4,32,1]{2,0,1,3:T(8,128)S(1)} %fusion.7), kind=kOutput, calls=%fused_computation.46 | convolution fusion | flops 18874368 | bytes 6500352 | tf_op jit(solution)/shard_map/shj,shje->she/dot_general | solution.py:68
  60.4 0.7 copy.47
  61.1 0.0 all-reduce.8.cloned.1.call-update
  61.1 0.0 all-reduce.10.cloned.1.call-start
  61.2 71.9 %all-reduce.8.cloned.1.call-done = f32[24,4,512]{2,0,1:T(8,128)} async-done(((f32[24,4,512]{2,0,1:T(8,128)}), f32[24,4,512]{2,0,1:T(8,128)}) %all-reduce.8.cloned.1.call-update) | async-done | bytes 196624 | tf_op jit(solution)/shard_map/psum | solution.py:71
  133.1 1.0 reduce_sum.55
  134.1 1.1 multiply_reduce_fusion
  135.2 0.0 copy-done
  135.2 0.0 copy-done.2
  135.2 0.0 copy-done.3
  135.2 0.0 copy-done.6
  135.3 3.8 %convolution_bitcast_fusion = f32[24,4096]{1,0:T(8,128)} fusion(bf16[4,64,4096]{2,1,0:T(8,128)(2,1)S(1)} %copy-done, bf16[4,64,4096]{2,1,0:T(8,128)(2,1)} %param.23, f32[24,4,512]{2,0,1:T(8,128)S(1)} %get-tuple-element.86, s32[]{:T(128)S(6)} %select_n.16, f32[4,64]{1,0:T(4,128)S(1)} %copy-done.6, f32[24,4]{0,1:T(4,128)S(1)} %add_rsqrt_fusion, ...), kind=kOutput, calls=%fused_computation.11 | convolution fusion | flops 101099520 | bytes 4854276 | tf_op jit(solution)/shard_map/shj,hjd->sd/dot_general | solution.py:80
  139.0 0.0 all-reduce.10.cloned.1.call-update
  139.0 0.0 all-reduce.12.cloned.1.call-start
  139.1 17.6 %all-reduce.10.cloned.1.call-done = f32[24,4096]{1,0:T(8,128)} async-done(((f32[24,4096]{1,0:T(8,128)}), f32[24,4096]{1,0:T(8,128)}) %all-reduce.10.cloned.1.call-update) | async-done | bytes 393232 | tf_op jit(solution)/shard_map/psum | solution.py:84
  156.6 0.0 all-reduce.12.cloned.1.call-update
  156.7 0.6 copy.38
  157.3 0.0 copy-done.8
  157.3 0.6 dynamic-slice
  158.6 0.0 copy-done.7
  158.6 74.4 %all-reduce.12.cloned.1.call-done = f32[24,4096]{1,0:T(8,128)} async-done(((f32[24,4096]{1,0:T(8,128)}), f32[24,4096]{1,0:T(8,128)}) %all-reduce.12.cloned.1.call-update) | async-done | bytes 393232 | tf_op jit(solution)/shard_map/psum | solution.py:84
  233.0 1.2 fusion.14
  234.2 0.0 copy-done.4
  234.2 8.3 %fusion.50 = (f32[24]{0:T(128)S(1)}, f32[24,1572]{1,0:T(8,128)S(1)}) fusion(bf16[1572,4096]{1,0:T(8,128)(2,1)} %param.29, bf16[24,4096]{1,0:T(8,128)(2,1)S(1)} %get-tuple-element.84, f32[4096]{0:T(1024)S(1)} %copy-done.4, f32[24]{0:T(128)S(1)} %add_rsqrt_fusion.1), kind=kOutput, calls=%fused_computation.74 | convolution fusion | flops 309498688 | bytes 13241920 | tf_op jit(solution)/shard_map/sd,vd->sv/dot_general | solution.py:88
  242.4 0.2 dynamic-update-slice
  242.7 0.2 select_reduce_fusion
  242.9 0.2 dynamic-update-slice.1
  243.1 0.2 dynamic-update-slice.2
  243.4 30.0 %all-reduce.3 = (f32[384]{0:T(512)S(1)}, f32[384]{0:T(512)S(1)}, f32[384]{0:T(512)S(1)}) all-reduce(f32[384]{0:T(512)S(1)} %dynamic-update-slice, f32[384]{0:T(512)S(1)} %dynamic-update-slice.1, f32[384]{0:T(512)S(1)} %dynamic-update-slice.2), channel_id=2, replica_groups=mesh['groups'=2,'row'=8,'head'=2] {'row','head'}, use_global_device_ids=true, to_apply=%add | all-reduce | flops 1152 | bytes 9216
  273.3 0.1 slice.36
  273.4 0.1 slice.37
  273.5 0.1 slice.38
  273.5 0.6 constant_dynamic-slice_fusion.3
  274.1 0.1 reshape.55
  274.2 0.1 reshape.56
  274.3 0.1 reshape.57
  274.4 0.6 while.14
  275.1 0.5 add_subtract_fusion
  (28 shorter events, 0.5 us)
Async XLA Ops:
  7.2 128.1 %copy-start = (bf16[4,64,4096]{2,1,0:T(8,128)(2,1)S(1)}, bf16[4,64,4096]{2,1,0:T(8,128)(2,1)}, u32[]{:S(2)}) copy-start(bf16[4,64,4096]{2,1,0:T(8,128)(2,1)} %param.24) | copy-start | bytes 6291460
  7.2 125.9 %all-reduce.8.cloned.1.call-start = ((), (), s32[]{:S(2)}) async-start(), calls=%async_computation | async-start | bytes 393216 | tf_op jit(solution)/shard_map/psum | solution.py:71
  46.6 7.9 %copy-start.5 = (f32[24,4]{0,1:T(4,128)}, f32[24,4]{0,1:T(4,128)S(1)}, u32[]{:S(2)}) copy-start(f32[24,4]{0,1:T(4,128)S(1)} %get-tuple-element.88) | copy-start | bytes 1156
  54.5 2.7 copy-start.1
  57.2 78.0 %copy-start.2 = (bf16[24,4096]{1,0:T(8,128)(2,1)S(1)}, bf16[24,4096]{1,0:T(8,128)(2,1)}, u32[]{:S(2)}) copy-start(bf16[24,4096]{1,0:T(8,128)(2,1)} %param.18) | copy-start | bytes 589828
  57.2 78.0 %copy-start.3 = (f32[4096]{0:T(1024)S(1)}, f32[4096]{0:T(1024)}, u32[]{:S(2)}) copy-start(f32[4096]{0:T(1024)} %param.19) | copy-start | bytes 49156
  57.2 78.1 %copy-start.6 = (f32[4,64]{1,0:T(4,128)S(1)}, f32[4,64]{1,0:T(4,128)}, u32[]{:S(2)}) copy-start(f32[4,64]{1,0:T(4,128)} %param.27) | copy-start | bytes 3076
  57.2 100.1 %copy-start.8 = (u32[32]{0:T(128)S(1)}, u32[32]{0:T(128)}, u32[]{:S(2)}) copy-start(u32[32]{0:T(128)} %constant.57) | copy-start | bytes 388
  57.2 101.4 %copy-start.7 = (s32[24]{0:T(128)S(1)}, s32[24]{0:T(128)}, u32[]{:S(2)}) copy-start(s32[24]{0:T(128)} %param.33) | copy-start | bytes 292
  57.2 176.9 %copy-start.4 = (f32[4096]{0:T(1024)S(1)}, f32[4096]{0:T(1024)}, u32[]{:S(2)}) copy-start(f32[4096]{0:T(1024)} %param.28) | copy-start | bytes 49156
  61.1 95.5 %all-reduce.10.cloned.1.call-start = ((), (), s32[]{:S(2)}) async-start(), calls=%async_computation.1 | async-start | bytes 786432 | tf_op jit(solution)/shard_map/psum | solution.py:84
  139.0 93.9 %all-reduce.12.cloned.1.call-start = ((), (), s32[]{:S(2)}) async-start(), calls=%async_computation.2 | async-start | bytes 786432 | tf_op jit(solution)/shard_map/psum | solution.py:84
Sparse Core Ops, SparseCore 0:
  61.2 71.7 all-reduce.7
  139.2 17.4 all-reduce.9
  160.0 72.9 all-reduce.11
